TPU v7x, 32 devices: a whole 2x2x4 slice. The times are simulated.
32 devices in a mesh: wide: 2 (over x), context: 4 (over z), tensor: 4 (over y, core).
Axes of the slice: x: 2, y: 2, z: 4, core: 2. Of those that a mesh axis runs over, the one named last changes fastest.
Arguments:
- layer_input: bfloat16 [96, 197, 768], P(('wide', 'tensor')), may hold values from -6 to 6
- qkv_weight: bfloat16 [768, 3, 768], P(('wide', 'tensor'), None, 'context'), may hold values from -0.21875 to 0.21875
- proj_weight: bfloat16 [768, 768], P('context', ('wide', 'tensor')), may hold values from -0.875 to 0.875
- norm_gains: bfloat16 [2, 768], P(None, ('wide', 'tensor')), may hold values from 0.5 to 1.5
- norm_biases: bfloat16 [2, 768], P(None, ('wide', 'tensor')), may hold values from -1.796875 to 1.796875
- router_keys: bfloat16 [768, 8], P(('wide', 'tensor')), may hold values from -0.21875 to 0.21875
- up_weight: bfloat16 [8, 768, 3072], P(('wide', 'context'), None, 'tensor'), may hold values from -0.4375 to 0.4375
- down_weight: bfloat16 [8, 3072, 768], P(('wide', 'context'), 'tensor'), may hold values from -0.4375 to 0.4375
- out_cotangent: bfloat16 [96, 197, 768], P(('wide', 'tensor')), may hold values from -6 to 6
Outputs:
- layer_output: bfloat16 [96, 197, 768], P(('wide', 'tensor'))
- rms_stats: float32 [96, 3], P(('wide', 'tensor'))
- input_grad: bfloat16 [96, 197, 768], P(('wide', 'tensor'))
- qkv_grad: float32 [768, 3, 768], P(('wide', 'tensor'), None, 'context')
- proj_grad: float32 [768, 768], P('context', ('wide', 'tensor'))
- gains_grad: float32 [2, 768], P(None, ('wide', 'tensor'))
- biases_grad: float32 [2, 768], P(None, ('wide', 'tensor'))
- router_grad: float32 [768, 8], P(('wide', 'tensor'))
- up_grad: float32 [8, 768, 3072], P(('wide', 'context'), None, 'tensor')
- down_grad: float32 [8, 3072, 768], P(('wide', 'context'), 'tensor')
All inputs are finite; a program needn't handle non-finite values.
Results may differ from a plain program's by a relative error of at most 0.02.
Values may be sent and summed in bfloat16 or wider, within the bound.
A program may use at most 192 MiB of HBM per device.

v0:
```python
import math
import jax
import jax.numpy as jnp
from jax import lax
from jax.sharding import PartitionSpec as P

HEAD_DIM = 64
norm_eps = 1e-06
highest = lax.Precision.HIGHEST
f32 = jnp.float32
bf16 = jnp.bfloat16


def layer_stats(values):
    center = values - jnp.mean(values, axis=-1, keepdims=True)
    spread = lax.rsqrt(jnp.mean(center * center, axis=-1, keepdims=True) + norm_eps)
    return (center * spread, spread)


def norm_back(upstream, scaled, spread):
    return spread * (
        upstream
        - jnp.mean(upstream, axis=-1, keepdims=True)
        - scaled * jnp.mean(upstream * scaled, axis=-1, keepdims=True)
    )


def root_mean(values):
    return jnp.sqrt(jnp.mean(values * values, axis=(1, 2)))


def dot32(spec, a, b, **kw):
    return jnp.einsum(spec, a, b, preferred_element_type=f32, **kw)


def on_device(
    layer_input,
    qkv_weight,
    proj_weight,
    norm_gains,
    norm_biases,
    router_keys,
    up_weight,
    down_weight,
    out_cotangent,
):
    images, length, width = layer_input.shape
    wide_n = lax.axis_size("wide")
    ctx_n = lax.axis_size("context")
    ten_n = lax.axis_size("tensor")
    share = images // ctx_n
    start = lax.axis_index("context") * share
    slots_n = router_keys.shape[1]
    cols = qkv_weight.shape[2]
    rows = qkv_weight.shape[0]
    heads_b = cols // HEAD_DIM
    logit_scale = 1.6 * math.sqrt(width)
    everyone = ("context", "wide", "tensor")
    plane = ("wide", "tensor")
    pack = jnp.concatenate([qkv_weight.reshape(rows, 3 * cols), proj_weight.T], axis=1)
    weights = lax.all_gather(pack, everyone, axis=0, tiled=True).reshape(ctx_n, width, 4 * cols)
    small = jnp.concatenate([norm_gains, norm_biases, router_keys.T], axis=0)
    small = lax.all_gather(small, plane, axis=1, tiled=True).astype(f32)
    gain_vals, bias_vals, router_vals = (small[0:2], small[2:4], small[4:].T)
    qkv_full = weights[:, :, : 3 * cols]
    proj_t = weights[:, :, 3 * cols :]
    x = lax.dynamic_slice_in_dim(layer_input, start, share, 0).astype(f32)
    g = lax.dynamic_slice_in_dim(out_cotangent, start, share, 0)
    hat1, spread1 = layer_stats(x)
    normed1 = (hat1 * gain_vals[0] + bias_vals[0]).astype(bf16)
    qkv = dot32("bld,cdk->cblk", normed1, qkv_full).astype(bf16)
    qkv = qkv.reshape(ctx_n, share, length, 3, heads_b, HEAD_DIM)
    q, k, v = (qkv[:, :, :, 0], qkv[:, :, :, 1], qkv[:, :, :, 2])
    scores = dot32("cbqhd,cbkhd->cbhqk", q, k) * 0.125
    top = jnp.max(scores, axis=-1, keepdims=True)
    exps = jnp.exp(scores - top)
    probs = exps / jnp.sum(exps, axis=-1, keepdims=True)
    probs_low = probs.astype(bf16)
    heads = dot32("cbhqk,cbkhd->cbqhd", probs_low, v).astype(bf16)
    heads = heads.reshape(ctx_n, share, length, cols)
    attention = dot32("cblh,ceh->ble", heads, proj_t)
    residual = x + attention
    hat2, spread2 = layer_stats(residual)
    second = hat2 * gain_vals[1] + bias_vals[1]
    tokens = second.astype(bf16)
    row_scale = lax.rsqrt(jnp.sum(second * second, axis=-1, keepdims=True) + norm_eps)
    unit = second * row_scale
    col_scale = lax.rsqrt(jnp.sum(router_vals * router_vals, axis=0, keepdims=True) + norm_eps)
    keys_unit = router_vals * col_scale
    logits = logit_scale * jnp.einsum("bld,ds->bls", unit, keys_unit, precision=highest)
    dispatch = jax.nn.softmax(logits, axis=1)
    combine = jax.nn.softmax(logits, axis=2)
    dispatch_low = dispatch.astype(bf16)
    combine_low = combine.astype(bf16)
    slots = dot32("bls,bld->sbd", dispatch_low, tokens).astype(bf16)
    dexp = dot32("bls,bld->sbd", combine_low, g).astype(bf16)
    out = jnp.concatenate([slots, dexp], axis=1)
    got = lax.all_to_all(out, ("wide", "context"), split_axis=0, concat_axis=0, tiled=True)
    got = lax.all_gather(got, "tensor", axis=0, tiled=True)
    n = got.shape[0]
    slot_all = got[:, :share].reshape(n * share, width)
    dexp_all = got[:, share:].reshape(n * share, width)
    up, down = (up_weight[0], down_weight[0])
    hidden = dot32("rd,df->rf", slot_all, up)
    active = jax.nn.gelu(hidden).astype(bf16)
    part_out = dot32("rf,fd->rd", active, down)
    active_grad = dot32("rd,fd->rf", dexp_all, down)
    hidden_grad = jax.vjp(jax.nn.gelu, hidden)[1](active_grad)[0].astype(bf16)
    down_grad = dot32("rf,rd->fd", active, dexp_all)[None]
    up_grad = dot32("rd,rf->df", slot_all, hidden_grad)[None]
    part_slot = dot32("rf,df->rd", hidden_grad, up)
    back = jnp.concatenate(
        [part_out.reshape(n, share, width), part_slot.reshape(n, share, width)], axis=1
    ).astype(bf16)
    back = lax.psum_scatter(back, "tensor", scatter_dimension=0, tiled=True)
    back = lax.all_to_all(back, ("wide", "context"), split_axis=0, concat_axis=0, tiled=True)
    expert_out = back[:, :share]
    dslots = back[:, share:]
    mixture = dot32("bls,sbd->bld", combine_low, expert_out)
    result = residual + mixture
    rms = jnp.stack([root_mean(result), root_mean(attention), root_mean(mixture)], axis=-1)
    layer_output = lax.all_gather(result.astype(bf16), "context", axis=0, tiled=True)
    dcomb = dot32("bld,sbd->bls", g, expert_out)
    ddisp = dot32("bld,sbd->bls", tokens, dslots)
    dtokens = dot32("bls,sbd->bld", dispatch_low, dslots)
    dlogits = combine * (dcomb - jnp.sum(combine * dcomb, axis=2, keepdims=True)) + dispatch * (
        ddisp - jnp.sum(dispatch * ddisp, axis=1, keepdims=True)
    )
    dunit = logit_scale * jnp.einsum("bls,ds->bld", dlogits, keys_unit, precision=highest)
    dkeys = logit_scale * jnp.einsum("bld,bls->ds", unit, dlogits, precision=highest)
    drouter = col_scale * (dkeys - keys_unit * jnp.sum(keys_unit * dkeys, axis=0, keepdims=True))
    dsecond = dtokens + row_scale * (dunit - unit * jnp.sum(unit * dunit, axis=-1, keepdims=True))
    dgain2 = jnp.sum(dsecond * hat2, axis=(0, 1))
    dbias2 = jnp.sum(dsecond, axis=(0, 1))
    dresid = g.astype(f32) + norm_back(dsecond * gain_vals[1], hat2, spread2)
    dattn = dresid.astype(bf16)
    dproj = dot32("ble,cblh->ceh", dattn, heads)
    dheads = dot32("ble,ceh->cblh", dattn, proj_t).astype(bf16)
    dheads = dheads.reshape(ctx_n, share, length, heads_b, HEAD_DIM)
    dprobs = dot32("cbqhd,cbkhd->cbhqk", dheads, v)
    dv = dot32("cbhqk,cbqhd->cbkhd", probs_low, dheads)
    ds = (probs * (dprobs - jnp.sum(probs * dprobs, axis=-1, keepdims=True))).astype(bf16)
    dq = dot32("cbhqk,cbkhd->cbqhd", ds, k) * 0.125
    dk = dot32("cbhqk,cbqhd->cbkhd", ds, q) * 0.125
    dqkv = jnp.stack([dq, dk, dv], axis=3).astype(bf16).reshape(ctx_n, share, length, 3 * cols)
    dqkv_w = dot32("bld,cblk->cdk", normed1, dqkv)
    dnormed1 = dot32("cblk,cdk->bld", dqkv, qkv_full)
    dgain1 = jnp.sum(dnormed1 * hat1, axis=(0, 1))
    dbias1 = jnp.sum(dnormed1, axis=(0, 1))
    dx = (dresid + norm_back(dnormed1 * gain_vals[0], hat1, spread1)).astype(bf16)
    input_grad = lax.all_gather(dx, "context", axis=0, tiled=True)
    rms = lax.all_gather(rms, "context", axis=0, tiled=True)
    dpack = jnp.concatenate([dqkv_w, dproj], axis=2).reshape(ctx_n * width, 4 * cols)
    dpack = lax.psum_scatter(dpack.astype(bf16), everyone, scatter_dimension=0, tiled=True)
    dpack = dpack.astype(f32)
    dsmall = jnp.concatenate([jnp.stack([dgain1, dgain2, dbias1, dbias2], axis=1), drouter], axis=1)
    dsmall = lax.psum(dsmall, "context")
    dsmall = lax.psum_scatter(dsmall, plane, scatter_dimension=0, tiled=True)
    return (
        layer_output,
        rms,
        input_grad,
        dpack[:, : 3 * cols].reshape(rows, 3, cols),
        dpack[:, 3 * cols :].T,
        dsmall[:, 0:2].T,
        dsmall[:, 2:4].T,
        dsmall[:, 4:],
        up_grad,
        down_grad,
    )


def solution(mesh):
    images = P(("wide", "tensor"), None, None)
    qkv = P(("wide", "tensor"), None, "context")
    proj = P("context", ("wide", "tensor"))
    lane = P(None, ("wide", "tensor"))
    rowed = P(("wide", "tensor"), None)
    up = P(("wide", "context"), None, "tensor")
    down = P(("wide", "context"), "tensor", None)
    return jax.shard_map(
        on_device,
        mesh=mesh,
        in_specs=(images, qkv, proj, lane, lane, rowed, up, down, images),
        out_specs=(images, rowed, images, qkv, proj, lane, lane, rowed, up, down),
        check_vma=False,
    )
```

profile of v0, /device:TPU:0, one launch (start us, length us, event | category | flops | bytes accessed | tf_op | source)
XLA Modules:
  0.0 542.7 jit_solution(13824113739327236245)
XLA Ops:
  10.8 10.6 %all-gather = bf16[8,96,12]{1,2,0:T(8,128)(2,1)S(1)} all-gather(bf16[1,96,12]{1,2,0:T(8,128)(2,1)S(1)} %maximum_bitcast_fusion.1), channel_id=1, replica_groups=mesh['wide'=2,'context'=4,'tensor'=4] {'wide','tensor'}, dimensions={0}, use_global_device_ids=true | all-gather | bytes 20736 | tf_op jit(solution)/shard_map/all_gather | solution.py:63
  24.8 53.0 %all-gather.6.cloned.1.call-done = bf16[3072,768]{1,0:T(8,128)(2,1)} async-done(((bf16[96,768]{1,0:T(8,128)(2,1)}), bf16[3072,768]{1,0:T(8,128)(2,1)}) %all-gather.6.cloned.1.call-update) | async-done | bytes 4718608 | tf_op jit(solution)/shard_map/all_gather | solution.py:61
  77.8 6.6 %convert_bitcast_fusion = bf16[4,3,197,576]{3,2,1,0:T(8,128)(2,1)} fusion(bf16[4,768,768]{2,1,0:T(8,128)(2,1)} %bitcast.228, f32[768]{0:T(1024)S(1)} %get-tuple-element.62, f32[768]{0:T(1024)S(1)} %get-tuple-element.63, f32[3,197]{1,0:T(4,128)S(1)} %add_rsqrt_fusion.2, f32[3,197]{1,0:T(4,128)S(1)} %broadcast_multiply_fusion.5, ...), kind=kOutput, calls=%fused_computation.16 | convolution fusion | flops 2095600896 | bytes 7587964 | tf_op jit(solution)/shard_map/bld,cdk->cblk/dot_general | solution.py:33
  84.4 5.8 %copy.124 = bf16[4,3,197,576]{2,3,1,0:T(8,128)(2,1)} copy(bf16[4,3,197,576]{3,2,1,0:T(8,128)(2,1)} %convert_bitcast_fusion) | data formatting | bytes 5446656 | tf_op jit(solution)/shard_map/convert_element_type | solution.py:71
  90.2 2.8 fusion.84
  93.0 6.5 %fusion.140 = (f32[4,3,3,197]{3,2,1,0:T(4,128)S(1)}, f32[4,3,3,197,197]{3,4,2,1,0:T(8,128)S(1)}) fusion(f32[4,3,3,197,197]{3,4,2,1,0:T(8,128)S(1)} %fusion.84), kind=kOutput, calls=%fused_computation.195 | output fusion | flops 5588692 | bytes 11205360 | tf_op jit(solution)/shard_map/sub | solution.py:76
  99.5 3.0 fusion.36
  102.6 4.7 fusion.137
  113.2 10.8 %all_to_all.10 = bf16[8,6,768]{2,1,0:T(8,128)(2,1)S(1)} all-to-all(bf16[8,6,768]{2,1,0:T(8,128)(2,1)S(1)} %copy.130), channel_id=1, replica_groups=mesh['wide'=2,'context'=4,'tensor'=4] {'wide','context'}, dimensions={0} | all-to-all | bytes 147456 | tf_op jit(solution)/shard_map/all_to_all | solution.py:98
  124.1 16.1 %all_gather.20 = bf16[32,6,768]{2,0,1:T(8,128)(2,1)S(1)} all-gather(bf16[8,6,768]{2,0,1:T(8,128)(2,1)S(1)} %copy.131), channel_id=1, replica_groups=mesh['wide'=2,'context'=4,'tensor'=4] {'tensor'}, dimensions={0}, use_global_device_ids=true | all-gather | bytes 368640 | tf_op jit(solution)/shard_map/all_gather | solution.py:99
  143.3 2.6 fusion.106
  152.2 16.8 %reduce-scatter.10.cloned.1.call-done = bf16[8,4608]{1,0:T(8,128)(2,1)} async-done(((bf16[32,4608]{1,0:T(8,128)(2,1)}), bf16[8,4608]{1,0:T(8,128)(2,1)}) %reduce-scatter.10.cloned.1.call-update) | async-done | bytes 73744
  169.9 12.6 %all_to_all.11 = bf16[8,6,768]{2,1,0:T(8,128)(2,1)S(1)} all-to-all(bf16[8,6,768]{2,1,0:T(8,128)(2,1)S(1)} %copy.136), channel_id=1, replica_groups=mesh['wide'=2,'context'=4,'tensor'=4] {'wide','context'}, dimensions={0} | all-to-all | bytes 147456 | tf_op jit(solution)/shard_map/all_to_all | solution.py:116
  184.8 2.2 fusion.119
  187.0 2.9 fusion.122
  193.4 11.0 %multiply_reduce_fusion.2 = (f32[768]{0:T(1024)}, f32[3,197]{1,0:T(4,128)S(1)}, f32[3,197]{1,0:T(4,128)S(1)}, f32[768]{0:T(1024)}, f32[3]{0:T(128)}, /*index=5*/...) fusion(f32[3,197,768]{2,1,0:T(8,128)S(1)} %get-tuple-element.65, f32[3,197]{1,0:T(4,128)S(1)} %copy-done.18, ...), kind=kOutput, calls=%fused_computation.44 | output fusion | flops 13615274 | bytes 10009668 | tf_op jit(solution)/shard_map/mul | solution.py:132
  206.5 4.0 convolution_convert_fusion
  210.6 5.2 multiply_reduce_fusion
  215.8 4.8 multiply_convert_fusion
  222.8 2.7 fusion.48
  228.4 7.0 %fusion.24 = (f32[768]{0:T(1024)S(1)}, f32[3,197]{1,0:T(4,128)S(1)}, f32[3,197]{1,0:T(4,128)S(1)}, f32[768]{0:T(1024)S(1)}, f32[3,197,768,1]{2,1,0,3:T(8,128)}) fusion(f32[3,197]{1,0:T(4,128)S(1)} %copy-done.26, f32[3,197]{1,0:T(4,128)S(1)} %copy-done.16, bf16[12,197,768]{2,1,0:T(8,128)(2,1)} %param.9, s32[]{:T(128)S(6)} %select_n.4, ...), kind=kOutput, calls=%fused_computation.38 | convolution fusion | flops 2096051968 | bytes 10217596 | tf_op jit(solution)/shard_map/cblk,cdk->bld/dot_general | solution.py:33
  236.8 3.3 fusion.23
  240.8 2.6 fusion.49
  243.4 5.1 fusion.8
  248.4 2.5 pad_maximum_fusion
  250.9 6.6 %copy.147 = bf16[4,768,768]{2,1,0:T(8,128)(2,1)} copy(bf16[4,768,768]{1,2,0:T(8,128)(2,1)} %pad_maximum_fusion) | data formatting | bytes 9437184 | tf_op jit(solution)/shard_map/concatenate | solution.py:153
  262.4 11.9 %all-gather.1 = f32[4,3,3]{2,1,0:T(4,128)S(1)} all-gather(f32[1,3,3]{2,1,0:T(4,128)S(1)} %bitcast.226), channel_id=1, replica_groups=mesh['wide'=2,'context'=4,'tensor'=4] {'context'}, dimensions={0}, use_global_device_ids=true | all-gather | bytes 180 | tf_op jit(solution)/shard_map/all_gather | solution.py:152
  276.0 9.0 %psum.8 = f32[96,12]{0,1:T(8,128)S(1)} all-reduce(f32[96,12]{0,1:T(8,128)S(1)} %copy.164), channel_id=1, replica_groups=mesh['wide'=2,'context'=4,'tensor'=4] {'context'}, use_global_device_ids=true, to_apply=%region_30.0 | all-reduce | flops 1152 | bytes 9216 | tf_op jit(solution)/shard_map/psum | solution.py:157
  286.1 55.5 %all-gather.10.cloned.1.call-done = bf16[12,197,768]{2,1,0:T(8,128)(2,1)} async-done(((bf16[3,197,768]{2,1,0:T(8,128)(2,1)}), bf16[12,197,768]{2,1,0:T(8,128)(2,1)}) %all-gather.10.cloned.1.call-update) | async-done | bytes 3631120 | tf_op jit(solution)/shard_map/all_gather | solution.py:151
  341.6 72.3 %all-gather.8.cloned.1.call-done = bf16[12,197,768]{2,1,0:T(8,128)(2,1)} async-done(((bf16[3,197,768]{2,1,0:T(8,128)(2,1)}), bf16[12,197,768]{2,1,0:T(8,128)(2,1)}) %all-gather.8.cloned.1.call-update) | async-done | bytes 3631120 | tf_op jit(solution)/shard_map/all_gather | solution.py:122
  414.0 111.4 %reduce-scatter.8.cloned.1.call-done = bf16[96,768]{1,0:T(8,128)(2,1)} async-done(((bf16[3072,768]{1,0:T(8,128)(2,1)}), bf16[96,768]{1,0:T(8,128)(2,1)}) %reduce-scatter.8.cloned.1.call-update) | async-done | bytes 147472 | tf_op jit(solution)/shard_map/reduce_scatter | solution.py:154
  529.1 4.3 copy.192
  (187 shorter events, 51.1 us)
Async XLA Ops:
  7.2 135.8 %copy-start = (bf16[1,768,768]{2,1,0:T(8,128)(2,1)S(1)}, bf16[1,768,768]{2,1,0:T(8,128)(2,1)}, u32[]{:S(2)}) copy-start(bf16[1,768,768]{2,1,0:T(8,128)(2,1)} %param.15) | copy-start | bytes 3538948
  7.2 70.6 %all-gather.6.cloned.1.call-start = ((), (), s32[]{:S(2)}) async-start(), calls=%async_computation.5 | async-start | bytes 4866048 | tf_op jit(solution)/shard_map/all_gather | solution.py:61
  10.1 159.0 %reduce-scatter.10.cloned.1.call-start = ((), (), s32[]{:S(2)}) async-start(), calls=%async_computation.9 | async-start | bytes 368640
  23.1 61.3 %copy-start.21 = (f32[768]{0:T(1024)}, f32[768]{0:T(1024)S(1)}, u32[]{:S(2)}) copy-start(f32[768]{0:T(1024)S(1)} %get-tuple-element.63) | copy-start | bytes 9220
  23.1 61.3 %copy-start.30 = (f32[768]{0:T(1024)}, f32[768]{0:T(1024)S(1)}, u32[]{:S(2)}) copy-start(f32[768]{0:T(1024)S(1)} %get-tuple-element.62) | copy-start | bytes 9220
  23.1 88.1 %copy-start.23 = (f32[768]{0:T(1024)}, f32[768]{0:T(1024)S(1)}, u32[]{:S(2)}) copy-start(f32[768]{0:T(1024)S(1)} %get-tuple-element.61) | copy-start | bytes 9220
  23.1 61.3 %copy-start.15 = (f32[3,197]{1,0:T(4,128)}, f32[3,197]{1,0:T(4,128)S(1)}, u32[]{:S(2)}) copy-start(f32[3,197]{1,0:T(4,128)S(1)} %broadcast_multiply_fusion.5) | copy-start | bytes 7096
  24.8 83.5 %copy-start.27 = (f32[8]{0:T(128)}, f32[8]{0:T(128)S(1)}, u32[]{:S(2)}) copy-start(f32[8]{0:T(128)S(1)} %add_rsqrt_fusion.3) | copy-start | bytes 100
  24.8 59.6 %copy-start.25 = (f32[3,197]{1,0:T(4,128)}, f32[3,197]{1,0:T(4,128)S(1)}, u32[]{:S(2)}) copy-start(f32[3,197]{1,0:T(4,128)S(1)} %add_rsqrt_fusion.2) | copy-start | bytes 7096
  102.6 4.8 copy-start.39
  151.3 32.8 %copy-start.14 = (f32[3,197,8]{1,2,0:T(8,128)S(1)}, f32[3,197,8]{1,2,0:T(8,128)}, u32[]{:S(2)}) copy-start(f32[3,197,8]{1,2,0:T(8,128)} %get-tuple-element.79) | copy-start | bytes 56740
  151.4 32.8 %copy-start.18 = (f32[3,197]{1,0:T(4,128)S(1)}, f32[3,197]{1,0:T(4,128)}, u32[]{:S(2)}) copy-start(f32[3,197]{1,0:T(4,128)} %copy-done.17) | copy-start | bytes 7096
  151.4 32.8 %copy-start.20 = (f32[3,8]{1,0:T(4,128)S(1)}, f32[3,8]{1,0:T(4,128)}, u32[]{:S(2)}) copy-start(f32[3,8]{1,0:T(4,128)} %copy-done.19) | copy-start | bytes 292
  151.4 32.8 %copy-start.24 = (f32[768]{0:T(1024)S(1)}, f32[768]{0:T(1024)}, u32[]{:S(2)}) copy-start(f32[768]{0:T(1024)} %copy-done.23) | copy-start | bytes 9220
  152.2 122.9 %reduce-scatter.12.cloned.1.call-start = ((), (), s32[]{:S(2)}) async-start(), calls=%async_computation.10 | async-start | bytes 442368
  204.4 6.1 %slice-start = ((s8[7372800]{0:T(1024)(128)(4,1)}), s8[4194304]{0:T(1024)(128)(4,1)S(1)}, s32[]{:S(2)}) async-start(s8[7372800]{0:T(1024)(128)(4,1)} %bitcast.205), calls=%async_computation.11 | async-start | bytes 8388608
  206.4 4.1 copy-start.4
  206.4 4.1 slice-start.1
  206.4 4.2 copy-start.3
  206.5 4.1 copy-start.13
  210.5 5.3 copy-start.40
  222.8 5.4 %slice-start.2 = ((s8[4718592]{0:T(1024)(128)(4,1)}), s8[4194304]{0:T(1024)(128)(4,1)S(1)}, s32[]{:S(2)}) async-start(s8[4718592]{0:T(1024)(128)(4,1)} %bitcast.231), calls=%async_computation.13 | async-start | bytes 8388608
  228.2 7.3 %copy-start.7 = (bf16[4,3,197,3,3,64]{2,5,4,3,1,0:T(8,128)(2,1)}, bf16[4,3,197,3,3,64]{2,5,4,3,1,0:T(8,128)(2,1)S(1)}, u32[]{:S(2)}) copy-start(bf16[4,3,197,3,3,64]{2,5,4,3,1,0:T(8,128)(2,1)S(1)} %copy.144) | copy-start | bytes 8169988
  228.4 7.1 %copy-start.33 = (f32[768]{0:T(1024)S(1)}, f32[768]{0:T(1024)}, u32[]{:S(2)}) copy-start(f32[768]{0:T(1024)} %get-tuple-element.52) | copy-start | bytes 9220
  228.4 7.1 %copy-start.32 = (f32[768]{0:T(1024)S(1)}, f32[768]{0:T(1024)}, u32[]{:S(2)}) copy-start(f32[768]{0:T(1024)} %get-tuple-element.56) | copy-start | bytes 9220
  228.4 7.1 %copy-start.29 = (f32[8]{0:T(128)S(1)}, f32[8]{0:T(128)}, u32[]{:S(2)}) copy-start(f32[8]{0:T(128)} %copy-done.27) | copy-start | bytes 100
  228.4 7.1 %copy-start.36 = (f32[8]{0:T(128)S(1)}, f32[8]{0:T(128)}, u32[]{:S(2)}) copy-start(f32[8]{0:T(128)} %get-tuple-element.90) | copy-start | bytes 100
  228.4 8.4 %copy-start.5 = (f32[3,197,768]{2,1,0:T(8,128)S(1)}, f32[3,197,768]{2,1,0:T(8,128)}, u32[]{:S(2)}) copy-start(f32[3,197,768]{2,1,0:T(8,128)} %copy-done.4) | copy-start | bytes 5446660
  236.7 104.9 %all-gather.10.cloned.1.call-start = ((), (), s32[]{:S(2)}) async-start(), calls=%async_computation.7 | async-start | bytes 4608000 | tf_op jit(solution)/shard_map/all_gather | solution.py:151
  240.1 173.8 %all-gather.8.cloned.1.call-start = ((), (), s32[]{:S(2)}) async-start(), calls=%async_computation.6 | async-start | bytes 4608000 | tf_op jit(solution)/shard_map/all_gather | solution.py:122
  240.7 284.6 %reduce-scatter.8.cloned.1.call-start = ((), (), s32[]{:S(2)}) async-start(), calls=%async_computation.8 | async-start | bytes 4866048 | tf_op jit(solution)/shard_map/reduce_scatter | solution.py:154
  529.1 4.3 copy-start.6
  (21 other events, 41.7 us)
Sparse Core Ops, SparseCore 0:
  11.5 66.2 all-gather.5
  152.3 16.6 reduce-scatter.9
  236.8 30.2 reduce-scatter.11
  269.1 72.4 all-gather.9
  343.0 70.8 all-gather.7
  419.3 106.0 reduce-scatter.7
where the time goes:
time: 552 us; the launch traced here: 543 us
  waiting for transfers between devices  310 us (56%)
  matrix products  72.2 us (13%)
  blocking collectives  71 us (13%)
  other arithmetic  38.7 us (7%)
  local copies, waits for them, and re-layouts  35.6 us (6%)
  between operations  15.3 us (3%)
    reduce_scatter x1, waiting for transfers between devices, on_device(): lax.psum_scatter(dpack.astype(bf16), everyone, scatter_dimension=0, tiled...  111 us
    all_gather x1, waiting for transfers between devices, on_device(): lax.all_gather(result.astype(bf16), 'context', axis=0, tiled=True)  72.3 us
    dot_general x24, matrix products, dot32(): return jnp.einsum(spec, a, b, preferred_element_type=f32, **kw)  65.1 us
    all_gather x1, waiting for transfers between devices, on_device(): input_grad = lax.all_gather(dx, 'context', axis=0, tiled=True)  55.5 us
    all_gather x1, waiting for transfers between devices, on_device(): lax.all_gather(pack, everyone, axis=0, tiled=True)  53 us
    unnamed x8, waiting for transfers between devices  17.4 us
    all_gather x1, blocking collectives, on_device(): got = lax.all_gather(got, 'tensor', axis=0, tiled=True)  16.1 us
    unnamed x103, local copies, waits for them, and re-layouts  13.7 us
  transfers between devices with their start and end apart: 6, of which 5 were waited for; matrix products, arithmetic and copies ran while one was open for 6% of the time, Pallas kernels for 0%

commit v1 on v0

--- a/solution.py
+++ b/solution.py
@@ -148,7 +148,14 @@
     dgain1 = jnp.sum(dnormed1 * hat1, axis=(0, 1))
     dbias1 = jnp.sum(dnormed1, axis=(0, 1))
     dx = (dresid + norm_back(dnormed1 * gain_vals[0], hat1, spread1)).astype(bf16)
-    input_grad = lax.all_gather(dx, "context", axis=0, tiled=True)
+    ways = lax.axis_size("context")
+    pieces = [dx]
+    for far in range(1, ways):
+        pieces.append(
+            lax.ppermute(pieces[far - 1], "context", [(d, (d - 1) % ways) for d in range(ways)])
+        )
+    line = jnp.concatenate(pieces, axis=0)
+    input_grad = jnp.roll(line, lax.axis_index("context") * dx.shape[0], axis=0)
     rms = lax.all_gather(rms, "context", axis=0, tiled=True)
     dpack = jnp.concatenate([dqkv_w, dproj], axis=2).reshape(ctx_n * width, 4 * cols)
     dpack = lax.psum_scatter(dpack.astype(bf16), everyone, scatter_dimension=0, tiled=True)

time: 552 us -> 515 us (0.933)
  waiting for transfers between devices: 310 us -> 233 us
  blocking collectives: 71 us -> 97.2 us
  local copies, waits for them, and re-layouts: 35.6 us -> 46.2 us
    ppermute x0 -> x3, waiting for transfers between devices: none -> 83.8 us  [on_device(): lax.ppermute(pieces[far - 1], 'context', [(d, (d - 1) % ways) for d in ra...]
    all_gather x1, waiting for transfers between devices: 72.3 us -> 0.01 us  [on_device(): lax.all_gather(result.astype(bf16), 'context', axis=0, tiled=True)]
    all_gather x1 -> x0, waiting for transfers between devices: 55.5 us -> none  [on_device(): input_grad = lax.all_gather(dx, 'context', axis=0, tiled=True)]
    reduce_scatter x1, waiting for transfers between devices: 111 us -> 79.1 us  [on_device(): lax.psum_scatter(dpack.astype(bf16), everyone, scatter_dimension=0, tiled...]
    all_gather x1, blocking collectives: 11.9 us -> 35.8 us  [on_device(): rms = lax.all_gather(rms, 'context', axis=0, tiled=True)]
    unnamed x103 -> x102, local copies, waits for them, and re-layouts: 13.7 us -> 17.8 us
    unnamed x8 -> x7, waiting for transfers between devices: 17.4 us -> 17.4 us
  transfers between devices with their start and end apart: 6 -> 8, of which waited for: 5 -> 5; matrix products, arithmetic and copies ran while one was open for 6% -> 9% of each run, Pallas kernels for 0% -> 0%
where the time goes in v1:
time: 515 us; the launch traced here: 506 us
  waiting for transfers between devices  233 us (45%)
  blocking collectives  97.2 us (19%)
  matrix products  72.7 us (14%)
  local copies, waits for them, and re-layouts  46.2 us (9%)
  other arithmetic  38.5 us (7%)
  between operations  15 us (3%)
    ppermute x3, waiting for transfers between devices, on_device(): lax.ppermute(pieces[far - 1], 'context', [(d, (d - 1) % ways) for d in ra...  83.8 us
    reduce_scatter x1, waiting for transfers between devices, on_device(): lax.psum_scatter(dpack.astype(bf16), everyone, scatter_dimension=0, tiled...  79.1 us
    dot_general x24, matrix products, dot32(): return jnp.einsum(spec, a, b, preferred_element_type=f32, **kw)  64.9 us
    all_gather x1, waiting for transfers between devices, on_device(): lax.all_gather(pack, everyone, axis=0, tiled=True)  53 us
    all_gather x1, blocking collectives, on_device(): rms = lax.all_gather(rms, 'context', axis=0, tiled=True)  35.8 us
    unnamed x102, local copies, waits for them, and re-layouts  17.8 us
    unnamed x7, waiting for transfers between devices  17.4 us
    all_gather x1, blocking collectives, on_device(): got = lax.all_gather(got, 'tensor', axis=0, tiled=True)  16.1 us
  transfers between devices with their start and end apart: 8, of which 5 were waited for; matrix products, arithmetic and copies ran while one was open for 9% of the time, Pallas kernels for 0%

profile of v1, /device:TPU:0, one launch (start us, length us, event | category | flops | bytes accessed | tf_op | source)
XLA Modules:
  0.0 505.6 jit_solution(13756609946605919613)
XLA Ops:
  10.8 10.6 %all-gather = bf16[8,96,12]{1,2,0:T(8,128)(2,1)S(1)} all-gather(bf16[1,96,12]{1,2,0:T(8,128)(2,1)S(1)} %maximum_bitcast_fusion.1), channel_id=1, replica_groups=mesh['wide'=2,'context'=4,'tensor'=4] {'wide','tensor'}, dimensions={0}, use_global_device_ids=true | all-gather | bytes 20736 | tf_op jit(solution)/shard_map/all_gather | solution.py:63
  24.8 53.0 %all-gather.5.cloned.1.call-done = bf16[3072,768]{1,0:T(8,128)(2,1)} async-done(((bf16[96,768]{1,0:T(8,128)(2,1)}), bf16[3072,768]{1,0:T(8,128)(2,1)}) %all-gather.5.cloned.1.call-update) | async-done | bytes 4718608 | tf_op jit(solution)/shard_map/all_gather | solution.py:61
  77.8 6.6 %convert_bitcast_fusion = bf16[4,3,197,576]{3,2,1,0:T(8,128)(2,1)} fusion(bf16[4,768,768]{2,1,0:T(8,128)(2,1)} %bitcast.229, f32[768]{0:T(1024)S(1)} %get-tuple-element.62, f32[768]{0:T(1024)S(1)} %get-tuple-element.63, f32[3,197]{1,0:T(4,128)S(1)} %add_rsqrt_fusion.2, f32[3,197]{1,0:T(4,128)S(1)} %broadcast_multiply_fusion.5, ...), kind=kOutput, calls=%fused_computation.16 | convolution fusion | flops 2095600896 | bytes 7587964 | tf_op jit(solution)/shard_map/bld,cdk->cblk/dot_general | solution.py:33
  84.4 5.8 %copy.124 = bf16[4,3,197,576]{2,3,1,0:T(8,128)(2,1)} copy(bf16[4,3,197,576]{3,2,1,0:T(8,128)(2,1)} %convert_bitcast_fusion) | data formatting | bytes 5446656 | tf_op jit(solution)/shard_map/convert_element_type | solution.py:71
  90.2 2.8 fusion.84
  93.0 6.5 %fusion.141 = (f32[4,3,3,197]{3,2,1,0:T(4,128)S(1)}, f32[4,3,3,197,197]{3,4,2,1,0:T(8,128)S(1)}) fusion(f32[4,3,3,197,197]{3,4,2,1,0:T(8,128)S(1)} %fusion.84), kind=kOutput, calls=%fused_computation.204 | output fusion | flops 5588692 | bytes 11205360 | tf_op jit(solution)/shard_map/sub | solution.py:76
  99.5 3.0 fusion.36
  102.6 4.7 fusion.138
  113.0 10.8 %all_to_all.10 = bf16[8,6,768]{2,1,0:T(8,128)(2,1)S(1)} all-to-all(bf16[8,6,768]{2,1,0:T(8,128)(2,1)S(1)} %copy.130), channel_id=1, replica_groups=mesh['wide'=2,'context'=4,'tensor'=4] {'wide','context'}, dimensions={0} | all-to-all | bytes 147456 | tf_op jit(solution)/shard_map/all_to_all | solution.py:98
  123.9 16.1 %all_gather.17 = bf16[32,6,768]{2,0,1:T(8,128)(2,1)S(1)} all-gather(bf16[8,6,768]{2,0,1:T(8,128)(2,1)S(1)} %copy.131), channel_id=1, replica_groups=mesh['wide'=2,'context'=4,'tensor'=4] {'tensor'}, dimensions={0}, use_global_device_ids=true | all-gather | bytes 368640 | tf_op jit(solution)/shard_map/all_gather | solution.py:99
  143.1 2.5 fusion.106
  152.0 16.8 %reduce-scatter.10.cloned.1.call-done = bf16[8,4608]{1,0:T(8,128)(2,1)} async-done(((bf16[32,4608]{1,0:T(8,128)(2,1)}), bf16[8,4608]{1,0:T(8,128)(2,1)}) %reduce-scatter.10.cloned.1.call-update) | async-done | bytes 73744
  169.7 12.6 %all_to_all.11 = bf16[8,6,768]{2,1,0:T(8,128)(2,1)S(1)} all-to-all(bf16[8,6,768]{2,1,0:T(8,128)(2,1)S(1)} %copy.136), channel_id=1, replica_groups=mesh['wide'=2,'context'=4,'tensor'=4] {'wide','context'}, dimensions={0} | all-to-all | bytes 147456 | tf_op jit(solution)/shard_map/all_to_all | solution.py:116
  184.7 2.9 fusion.119
  187.5 2.9 fusion.122
  193.9 10.9 %multiply_reduce_fusion.2 = (f32[768]{0:T(1024)S(1)}, f32[3,197]{1,0:T(4,128)S(1)}, f32[3,197]{1,0:T(4,128)S(1)}, f32[768]{0:T(1024)S(1)}, f32[3]{0:T(128)}, /*i...) fusion(f32[3,197,768]{2,1,0:T(8,128)S(1)} %get-tuple-element.67, f32[3,197]{1,0:T(4,128)S(1)} %copy-done.16, ...), kind=kOutput, calls=%fused_computation.44 | output fusion | flops 13615274 | bytes 10009668 | tf_op jit(solution)/shard_map/mul | solution.py:132
  206.9 4.0 convolution_convert_fusion
  211.0 5.2 %multiply_reduce_fusion = (f32[4,3,3,197]{3,2,1,0:T(4,128)}, f32[4,3,3,197,197]{3,4,2,1,0:T(8,128)}) fusion(f32[4,3,3,197,197]{3,4,2,1,0:T(8,128)S(1)} %bitcast.207, f32[4,3,3,197]{3,2,1,0:T(4,128)S(1)} %copy-done.12, bf16[4,3,197,3,64]{2,4,3,1,0:T(8,128)(2,1)S(1)} %bitcast.237, bf16[4,3,197,3,3,64]{2,5,4,3,1,0:T(8,128)(2,1)S(1)} %bitcast.212), kind=kOutput, calls=%fused_computation.5 | convolution fusion | flops 183016144 | bytes 15398112 | tf_op jit(solution)/shard_map/cbqhd,cbkhd->cbhqk/dot_general | solution.py:33
  216.2 4.8 multiply_convert_fusion
  223.1 2.7 fusion.48
  228.8 6.9 %fusion.24 = (f32[768]{0:T(1024)S(1)}, f32[3,197]{1,0:T(4,128)S(1)}, f32[3,197]{1,0:T(4,128)S(1)}, f32[768]{0:T(1024)S(1)}, f32[3,197,768,1]{2,1,0,3:T(8,128)}) fusion(f32[3,197]{1,0:T(4,128)S(1)} %copy-done.25, f32[3,197]{1,0:T(4,128)S(1)} %copy-done.14, bf16[12,197,768]{2,1,0:T(8,128)(2,1)} %param.9, s32[]{:T(128)S(6)} %select_n.17, ...), kind=kOutput, calls=%fused_computation.38 | convolution fusion | flops 2096051968 | bytes 10217596 | tf_op jit(solution)/shard_map/cblk,cdk->bld/dot_general | solution.py:33
  237.6 2.6 fusion.49
  240.2 5.1 fusion.8
  247.6 6.6 %copy.147 = bf16[4,768,768]{2,1,0:T(8,128)(2,1)} copy(bf16[4,768,768]{1,2,0:T(8,128)(2,1)} %pad_maximum_fusion) | data formatting | bytes 9437184 | tf_op jit(solution)/shard_map/concatenate | solution.py:160
  254.4 3.4 constant_dynamic-update-slice_fusion.7
  258.2 20.2 %collective-permute-done = bf16[3,197,768]{2,1,0:T(8,128)(2,1)S(1)} collective-permute-done((bf16[3,197,768]{2,1,0:T(8,128)(2,1)S(1)}, bf16[3,197,768]{2,1,0:T(8,128)(2,1)S(1)}, u32[]{:S(2)}, u32[]{:S(2)}) %collective-permute-start) | collective-permute-done | bytes 907808 | tf_op jit(solution)/shard_map/ppermute | solution.py:155
  282.5 63.6 %collective-permute-done.1 = bf16[3,197,768]{2,1,0:T(8,128)(2,1)S(1)} collective-permute-done((bf16[3,197,768]{2,1,0:T(8,128)(2,1)S(1)}, bf16[3,197,768]{2,1,0:T(8,128)(2,1)S(1)}, u32[]{:S(2)}, u32[]{:S(2)}) %collective-permute-start.1) | collective-permute-done | bytes 907808 | tf_op jit(solution)/shard_map/ppermute | solution.py:155
  348.1 35.8 %all-gather.1 = f32[4,3,3]{2,1,0:T(4,128)S(1)} all-gather(f32[1,3,3]{2,1,0:T(4,128)S(1)} %bitcast.227), channel_id=1, replica_groups=mesh['wide'=2,'context'=4,'tensor'=4] {'context'}, dimensions={0}, use_global_device_ids=true | all-gather | bytes 180 | tf_op jit(solution)/shard_map/all_gather | solution.py:159
  385.5 11.3 %psum.8 = f32[96,12]{0,1:T(8,128)S(1)} all-reduce(f32[96,12]{0,1:T(8,128)S(1)} %copy.164), channel_id=1, replica_groups=mesh['wide'=2,'context'=4,'tensor'=4] {'context'}, use_global_device_ids=true, to_apply=%region_30.31 | all-reduce | flops 1152 | bytes 9216 | tf_op jit(solution)/shard_map/psum | solution.py:164
  407.4 4.2 constant_dynamic-slice_fusion
  411.6 79.1 %reduce-scatter.8.cloned.1.call-done = bf16[96,768]{1,0:T(8,128)(2,1)} async-done(((bf16[3072,768]{1,0:T(8,128)(2,1)}), bf16[96,768]{1,0:T(8,128)(2,1)}) %reduce-scatter.8.cloned.1.call-update) | async-done | bytes 147472 | tf_op jit(solution)/shard_map/reduce_scatter | solution.py:161
  494.5 4.2 copy.198
  (191 shorter events, 62.3 us)
Async XLA Ops:
  7.2 135.6 %copy-start = (bf16[1,768,768]{2,1,0:T(8,128)(2,1)S(1)}, bf16[1,768,768]{2,1,0:T(8,128)(2,1)}, u32[]{:S(2)}) copy-start(bf16[1,768,768]{2,1,0:T(8,128)(2,1)} %param.15) | copy-start | bytes 3538948
  7.2 70.6 %all-gather.5.cloned.1.call-start = ((), (), s32[]{:S(2)}) async-start(), calls=%async_computation.5 | async-start | bytes 4866048 | tf_op jit(solution)/shard_map/all_gather | solution.py:61
  10.1 158.8 %reduce-scatter.10.cloned.1.call-start = ((), (), s32[]{:S(2)}) async-start(), calls=%async_computation.8 | async-start | bytes 368640
  23.1 61.3 %copy-start.20 = (f32[768]{0:T(1024)}, f32[768]{0:T(1024)S(1)}, u32[]{:S(2)}) copy-start(f32[768]{0:T(1024)S(1)} %get-tuple-element.63) | copy-start | bytes 9220
  23.1 61.3 %copy-start.29 = (f32[768]{0:T(1024)}, f32[768]{0:T(1024)S(1)}, u32[]{:S(2)}) copy-start(f32[768]{0:T(1024)S(1)} %get-tuple-element.62) | copy-start | bytes 9220
  23.1 87.9 %copy-start.22 = (f32[768]{0:T(1024)}, f32[768]{0:T(1024)S(1)}, u32[]{:S(2)}) copy-start(f32[768]{0:T(1024)S(1)} %get-tuple-element.61) | copy-start | bytes 9220
  23.1 61.3 %copy-start.13 = (f32[3,197]{1,0:T(4,128)}, f32[3,197]{1,0:T(4,128)S(1)}, u32[]{:S(2)}) copy-start(f32[3,197]{1,0:T(4,128)S(1)} %broadcast_multiply_fusion.5) | copy-start | bytes 7096
  24.8 83.5 %copy-start.26 = (f32[8]{0:T(128)}, f32[8]{0:T(128)S(1)}, u32[]{:S(2)}) copy-start(f32[8]{0:T(128)S(1)} %add_rsqrt_fusion.3) | copy-start | bytes 100
  24.8 59.6 %copy-start.24 = (f32[3,197]{1,0:T(4,128)}, f32[3,197]{1,0:T(4,128)S(1)}, u32[]{:S(2)}) copy-start(f32[3,197]{1,0:T(4,128)S(1)} %add_rsqrt_fusion.2) | copy-start | bytes 7096
  102.6 4.8 copy-start.36
  151.1 32.8 %copy-start.16 = (f32[3,197]{1,0:T(4,128)S(1)}, f32[3,197]{1,0:T(4,128)}, u32[]{:S(2)}) copy-start(f32[3,197]{1,0:T(4,128)} %copy-done.15) | copy-start | bytes 7096
  151.2 32.8 %copy-start.19 = (f32[3,8]{1,0:T(4,128)S(1)}, f32[3,8]{1,0:T(4,128)}, u32[]{:S(2)}) copy-start(f32[3,8]{1,0:T(4,128)} %copy-done.18) | copy-start | bytes 292
  151.2 32.8 %copy-start.23 = (f32[768]{0:T(1024)S(1)}, f32[768]{0:T(1024)}, u32[]{:S(2)}) copy-start(f32[768]{0:T(1024)} %copy-done.22) | copy-start | bytes 9220
  152.0 232.7 %reduce-scatter.12.cloned.1.call-start = ((), (), s32[]{:S(2)}) async-start(), calls=%async_computation.9 | async-start | bytes 442368
  204.8 6.1 %slice-start = ((s8[7372800]{0:T(1024)(128)(4,1)}), s8[4194304]{0:T(1024)(128)(4,1)S(1)}, s32[]{:S(2)}) async-start(s8[7372800]{0:T(1024)(128)(4,1)} %bitcast.206), calls=%async_computation.10 | async-start | bytes 8388608
  210.9 5.3 %copy-start.37 = (bf16[4,192,3,197]{3,1,2,0:T(8,128)(2,1)}, bf16[4,192,3,197]{3,1,2,0:T(8,128)(2,1)S(1)}, u32[]{:S(2)}) copy-start(bf16[4,192,3,197]{3,1,2,0:T(8,128)(2,1)S(1)} %convolution_convert_fusion) | copy-start | bytes 2723332
  223.1 5.5 %slice-start.2 = ((s8[4718592]{0:T(1024)(128)(4,1)}), s8[4194304]{0:T(1024)(128)(4,1)S(1)}, s32[]{:S(2)}) async-start(s8[4718592]{0:T(1024)(128)(4,1)} %bitcast.232), calls=%async_computation.12 | async-start | bytes 8388608
  228.6 7.1 %copy-start.6 = (bf16[4,3,197,3,3,64]{2,5,4,3,1,0:T(8,128)(2,1)}, bf16[4,3,197,3,3,64]{2,5,4,3,1,0:T(8,128)(2,1)S(1)}, u32[]{:S(2)}) copy-start(bf16[4,3,197,3,3,64]{2,5,4,3,1,0:T(8,128)(2,1)S(1)} %copy.144) | copy-start | bytes 8169988
  228.8 6.9 %copy-start.17 = (f32[768,8]{0,1:T(8,128)S(1)}, f32[768,8]{0,1:T(8,128)}, u32[]{:S(2)}) copy-start(f32[768,8]{0,1:T(8,128)} %get-tuple-element.93) | copy-start | bytes 73732
  228.8 6.9 %copy-start.28 = (f32[8]{0:T(128)S(1)}, f32[8]{0:T(128)}, u32[]{:S(2)}) copy-start(f32[8]{0:T(128)} %copy-done.26) | copy-start | bytes 100
  228.8 6.9 %copy-start.33 = (f32[8]{0:T(128)S(1)}, f32[8]{0:T(128)}, u32[]{:S(2)}) copy-start(f32[8]{0:T(128)} %get-tuple-element.92) | copy-start | bytes 100
  236.9 174.7 %all-gather.7.cloned.1.call-start = ((), (), s32[]{:S(2)}) async-start(), calls=%async_computation.6 | async-start | bytes 4608000 | tf_op jit(solution)/shard_map/all_gather | solution.py:122
  237.5 253.3 %reduce-scatter.8.cloned.1.call-start = ((), (), s32[]{:S(2)}) async-start(), calls=%async_computation.7 | async-start | bytes 4866048 | tf_op jit(solution)/shard_map/reduce_scatter | solution.py:161
  254.3 26.3 %copy-start.39 = (f32[3]{0:T(128)S(1)}, f32[3]{0:T(128)}, u32[]{:S(2)}) copy-start(f32[3]{0:T(128)} %get-tuple-element.69) | copy-start | bytes 40
  254.3 26.3 %copy-start.10 = (bf16[96,768]{1,0:T(8,128)(2,1)S(1)}, bf16[96,768]{1,0:T(8,128)(2,1)}, u32[]{:S(2)}) copy-start(bf16[96,768]{1,0:T(8,128)(2,1)} %fusion.106) | copy-start | bytes 442372
  257.8 88.3 %copy-start.9 = (bf16[96,768]{1,0:T(8,128)(2,1)S(1)}, bf16[96,768]{1,0:T(8,128)(2,1)}, u32[]{:S(2)}) copy-start(bf16[96,768]{1,0:T(8,128)(2,1)} %reshape.164) | copy-start | bytes 442372
  257.8 20.6 %collective-permute-start = (bf16[3,197,768]{2,1,0:T(8,128)(2,1)S(1)}, bf16[3,197,768]{2,1,0:T(8,128)(2,1)S(1)}, u32[]{:S(2)}, u32[]{:S(2)}) collective-permute-start(bf16[3,197,768]{2,1,0:T(8,128)(2,1)S(1)} %get-tuple-element.65), channel_id=1, source_target_pairs={{0,12},{4,0},{8,4},{12,8},{1,13},{5,1},{9,5},{13,9},{2,14},{6,2},{... | collective-permute-start | bytes 2723336 | tf_op jit(solution)/shard_map/ppermute | solution.py:155
  278.4 67.7 %collective-permute-start.1 = (bf16[3,197,768]{2,1,0:T(8,128)(2,1)S(1)}, bf16[3,197,768]{2,1,0:T(8,128)(2,1)S(1)}, u32[]{:S(2)}, u32[]{:S(2)}) collective-permute-start(bf16[3,197,768]{2,1,0:T(8,128)(2,1)S(1)} %collective-permute-done), channel_id=1, source_target_pairs={{0,12},{4,0},{8,4},{12,8},{1,13},{5,1},{9,5},{13,9},{2,14},{6,2},{... | collective-permute-start | bytes 2723336 | tf_op jit(solution)/shard_map/ppermute | solution.py:155
  282.5 65.5 %copy-start.34 = (f32[3]{0:T(128)S(1)}, f32[3]{0:T(128)}, u32[]{:S(2)}) copy-start(f32[3]{0:T(128)} %get-tuple-element.57) | copy-start | bytes 40
  282.5 65.5 %copy-start.35 = (f32[3]{0:T(128)S(1)}, f32[3]{0:T(128)}, u32[]{:S(2)}) copy-start(f32[3]{0:T(128)} %get-tuple-element.58) | copy-start | bytes 40
  346.1 53.9 %collective-permute-start.2 = (bf16[3,197,768]{2,1,0:T(8,128)(2,1)S(1)}, bf16[3,197,768]{2,1,0:T(8,128)(2,1)}, u32[]{:S(2)}, u32[]{:S(2)}) collective-permute-start(bf16[3,197,768]{2,1,0:T(8,128)(2,1)S(1)} %collective-permute-done.1), channel_id=1, source_target_pairs={{0,12},{4,0},{8,4},{12,8},{1,13},{5,1},{9,5},{13,9},{2,14},{6,2},{... | collective-permute-start | bytes 2723336 | tf_op jit(solution)/shard_map/ppermute | solution.py:155
  494.5 4.2 copy-start.1
  (20 other events, 49.7 us)
Sparse Core Ops, SparseCore 0:
  11.5 66.2 all-gather.4
  152.1 16.7 reduce-scatter.9
  237.0 30.2 reduce-scatter.11
  268.7 104.8 all-gather.6
  379.0 111.7 reduce-scatter.7
